TPU v7x, 512 devices: a 8x2x16 block of a 8x8x16 slice. The times are simulated.
512 devices in a mesh: groups: 2 (over y), mp: 16 (over z), dp: 8 (over x), guide: 2 (over core).
Axes of the slice: x: 8, y: 2, z: 16, core: 2. Of those that a mesh axis runs over, the one named last changes fastest.
The devices are a block of a 8x8x16 slice.
Arguments:
- tokens: bfloat16 [768, 8192], P(('groups', 'mp'), ('dp', 'guide')), parts along dimension 0, may hold values from -6 to 6
- w_gate: bfloat16 [8192, 14336], P(('dp', 'guide'), 'mp'), may hold values from -0.0625 to 0.0625
- w_up: bfloat16 [8192, 14336], P(('dp', 'guide'), 'mp'), may hold values from -0.0625 to 0.0625
- w_down: bfloat16 [14336, 8192], P('mp', ('dp', 'guide')), may hold values from -0.046875 to 0.046875
Outputs:
- layer_output: bfloat16 [768, 8192], P(('groups', 'mp'), ('dp', 'guide')), parts along dimension 0
There are 2 independent parts, one for each index of `groups`. A program takes and returns all parts, laid end to end along the dimension named above; an argument that names none is the same for every part. Nothing has to cross between parts.
All inputs are finite; a program needn't handle non-finite values.
Results may differ from a plain program's by a relative error of at most 0.0049.
Values may be sent and summed in bfloat16 or wider, within the bound.
No kernel may reach another device: no remote copies, remote signals or barrier semaphores. Data moves between devices by JAX's collectives and lax.ppermute only.
A program may use at most 64 MiB of HBM per device.

v0:
```python
import jax
import jax.numpy as jnp
from jax import lax
from jax.sharding import PartitionSpec as P


def summed_on_arrival(tiles, axis):
    arrived = lax.all_to_all(tiles, axis, split_axis=0, concat_axis=0, tiled=True)
    return arrived.astype(jnp.float32).sum(axis=0)


def cut(shard, count):
    return shard.reshape(count, shard.shape[0] // count, *shard.shape[1:])


def per_device(tokens, w_gate, w_up, w_down):
    columns = w_gate.shape[1]
    mp, dp, guide = (lax.axis_size(axis) for axis in ("mp", "dp", "guide"))
    paired_weights = jnp.concatenate([w_gate, w_up], axis=1)
    blocks = lax.all_gather(tokens, "mp", axis=0, tiled=False)
    blocks = blocks.reshape(dp, guide, -1, *tokens.shape)
    gathered = blocks.swapaxes(0, 1).reshape(-1, tokens.shape[1])
    partial_terms = jnp.dot(gathered, paired_weights, preferred_element_type=jnp.float32)
    chip_terms = summed_on_arrival(cut(partial_terms, guide), "guide").astype(jnp.bfloat16)
    summed = summed_on_arrival(cut(chip_terms, dp), "dp")
    hidden_share = (jax.nn.silu(summed[:, :columns]) * summed[:, columns:]).astype(jnp.bfloat16)
    hidden = lax.all_gather(hidden_share, ("dp", "guide"), axis=0, tiled=True)
    output_terms = jnp.dot(hidden, w_down, preferred_element_type=jnp.float32).astype(jnp.bfloat16)
    return summed_on_arrival(cut(output_terms, mp), "mp").astype(jnp.bfloat16)


def solution(mesh):
    placed = (
        P(("groups", "mp"), ("dp", "guide")),
        P(("dp", "guide"), "mp"),
        P(("dp", "guide"), "mp"),
        P("mp", ("dp", "guide")),
    )
    return jax.shard_map(
        per_device,
        mesh=mesh,
        in_specs=placed,
        out_specs=P(("groups", "mp"), ("dp", "guide")),
        check_vma=False,
    )
```

profile of v0, /device:TPU:80, one launch (start us, length us, event | category | flops | bytes accessed | tf_op | source)
XLA Modules:
  0.0 155.5 jit_solution(7631162222626804880)
XLA Ops:
  0.0 0.0 copy-start
  0.0 70.5 %all-gather = bf16[384,512]{1,0:T(8,128)(2,1)S(1)} all-gather(bf16[24,512]{1,0:T(8,128)(2,1)} %param.4), channel_id=2, replica_groups=mesh['groups'=2,'mp'=16,'dp'=8,'guide'=2] {'mp'}, dimensions={0}, use_global_device_ids=true | all-gather | bytes 417792 | tf_op jit(solution)/shard_map/all_gather | solution.py:20
  70.6 2.3 %fusion = f32[1792,384]{0,1:T(8,128)S(1)} fusion(bf16[384,512]{1,0:T(8,128)(2,1)S(1)} %bitcast.14, bf16[512,896]{1,0:T(8,128)(2,1)} %param.6, bf16[512,896]{1,0:T(8,128)(2,1)} %param.5), kind=kOutput, calls=%fused_computation | convolution fusion | flops 708313088 | bytes 4980736 | tf_op jit(solution)/shard_map/dot_general | solution.py:23
  72.9 6.9 %all_to_all.15 = f32[2,192,1792]{2,1,0:T(8,128)} all-to-all(f32[2,192,1792]{2,1,0:T(8,128)S(1)} %bitcast.12), channel_id=1, replica_groups=mesh['groups'=2,'mp'=16,'dp'=8,'guide'=2] {'guide'}, dimensions={0} | all-to-all | bytes 5505024 | tf_op jit(solution)/shard_map/all_to_all | solution.py:8
  79.8 2.0 %reduce_sum.30 = bf16[192,1792]{1,0:T(8,128)(2,1)S(1)} reduce(f32[2,192,1792]{2,1,0:T(8,128)} %all_to_all.15, f32[]{:T(128)} %constant.4.clone.1), dimensions={0}, to_apply=%region_0.0 | reduce | flops 344064 | bytes 3440644 | tf_op jit(solution)/shard_map/reduce_sum | solution.py:9
  81.8 28.4 %all_to_all.16 = bf16[8,24,1792]{2,1,0:T(8,128)(2,1)S(1)} all-to-all(bf16[8,24,1792]{2,1,0:T(8,128)(2,1)S(1)} %bitcast.13), channel_id=1, replica_groups=mesh['groups'=2,'mp'=16,'dp'=8,'guide'=2] {'dp'}, dimensions={0} | all-to-all | bytes 1376256 | tf_op jit(solution)/shard_map/all_to_all | solution.py:8
  110.2 0.1 convert_reduce_fusion
  110.4 16.6 %all_gather.11 = bf16[384,896]{1,0:T(8,128)(2,1)S(1)} all-gather(bf16[24,896]{1,0:T(8,128)(2,1)S(1)} %fusion.4), channel_id=1, replica_groups=mesh['groups'=2,'mp'=16,'dp'=8,'guide'=2] {'dp','guide'}, dimensions={0}, use_global_device_ids=true | all-gather | bytes 731136 | tf_op jit(solution)/shard_map/all_gather | solution.py:27
  127.0 0.0 copy-done
  127.0 0.6 convolution_convert_fusion
  127.6 27.3 %all_to_all.17 = bf16[16,24,512]{2,1,0:T(8,128)(2,1)S(1)} all-to-all(bf16[16,24,512]{2,1,0:T(8,128)(2,1)S(1)} %bitcast.16), channel_id=1, replica_groups=mesh['groups'=2,'mp'=16,'dp'=8,'guide'=2] {'mp'}, dimensions={0} | all-to-all | bytes 786432 | tf_op jit(solution)/shard_map/all_to_all | solution.py:8
  154.9 0.7 reduce_sum.32
  (2 shorter events, 0.1 us)
Async XLA Ops:
  0.0 127.0 %copy-start = (bf16[896,512]{1,0:T(8,128)(2,1)S(1)}, bf16[896,512]{1,0:T(8,128)(2,1)}, u32[]{:S(2)}) copy-start(bf16[896,512]{1,0:T(8,128)(2,1)} %param.7) | copy-start | bytes 2752516
where the time goes:
time: 156 us
  blocking collectives  150 us (96%)
  matrix products  2.91 us (2%)
  other arithmetic  2.8 us (2%)
    all_gather x1, blocking collectives, per_device(): blocks = lax.all_gather(tokens, 'mp', axis=0, tiled=False)  70.5 us
    all_to_all x3, blocking collectives, summed_on_arrival(): lax.all_to_all(tiles, axis, split_axis=0, concat_axis=0, tiled=True)  62.6 us
    all_gather x1, blocking collectives, per_device(): hidden = lax.all_gather(hidden_share, ('dp', 'guide'), axis=0, tiled=True)  16.6 us

commit v1 on v0

--- a/solution.py
+++ b/solution.py
@@ -24,7 +24,12 @@
     chip_terms = summed_on_arrival(cut(partial_terms, guide), "guide").astype(jnp.bfloat16)
     summed = summed_on_arrival(cut(chip_terms, dp), "dp")
     hidden_share = (jax.nn.silu(summed[:, :columns]) * summed[:, columns:]).astype(jnp.bfloat16)
-    hidden = lax.all_gather(hidden_share, ("dp", "guide"), axis=0, tiled=True)
+    hidden = jnp.concatenate(
+        lax.all_to_all(
+            jnp.stack([hidden_share] * lax.axis_size(("dp", "guide"))), ("dp", "guide"), 0, 0
+        ),
+        axis=0,
+    )
     output_terms = jnp.dot(hidden, w_down, preferred_element_type=jnp.float32).astype(jnp.bfloat16)
     return summed_on_arrival(cut(output_terms, mp), "mp").astype(jnp.bfloat16)
 

time: 156 us -> 164 us (1.051)
  blocking collectives: 150 us -> 158 us
    all_to_all x0 -> x1, blocking collectives: none -> 23.2 us  [per_device(): lax.all_to_all(jnp.stack([hidden_share] * lax.axis_size(('dp', 'guide')))...]
    all_gather x1 -> x0, blocking collectives: 16.6 us -> none  [per_device(): hidden = lax.all_gather(hidden_share, ('dp', 'guide'), axis=0, tiled=True)]
    all_to_all x3, blocking collectives: 62.6 us -> 64.2 us  [summed_on_arrival(): lax.all_to_all(tiles, axis, split_axis=0, concat_axis=0, tiled=True)]
where the time goes in v1:
time: 164 us
  blocking collectives  158 us (96%)
  matrix products  2.91 us (2%)
  other arithmetic  2.8 us (2%)
    all_gather x1, blocking collectives, per_device(): blocks = lax.all_gather(tokens, 'mp', axis=0, tiled=False)  70.5 us
    all_to_all x3, blocking collectives, summed_on_arrival(): lax.all_to_all(tiles, axis, split_axis=0, concat_axis=0, tiled=True)  64.2 us
    all_to_all x1, blocking collectives, per_device(): lax.all_to_all(jnp.stack([hidden_share] * lax.axis_size(('dp', 'guide')))...  23.2 us

profile of v1, /device:TPU:80, one launch (start us, length us, event | category | flops | bytes accessed | tf_op | source)
XLA Modules:
  0.0 163.8 jit_solution(2736902151666224511)
XLA Ops:
  0.0 0.0 copy-start
  0.0 70.5 %all-gather = bf16[384,512]{1,0:T(8,128)(2,1)S(1)} all-gather(bf16[24,512]{1,0:T(8,128)(2,1)} %param.4), channel_id=2, replica_groups=mesh['groups'=2,'mp'=16,'dp'=8,'guide'=2] {'mp'}, dimensions={0}, use_global_device_ids=true | all-gather | bytes 417792 | tf_op jit(solution)/shard_map/all_gather | solution.py:20
  70.6 2.3 %fusion = f32[1792,384]{0,1:T(8,128)S(1)} fusion(bf16[384,512]{1,0:T(8,128)(2,1)S(1)} %bitcast.15, bf16[512,896]{1,0:T(8,128)(2,1)} %param.6, bf16[512,896]{1,0:T(8,128)(2,1)} %param.5), kind=kOutput, calls=%fused_computation | convolution fusion | flops 708313088 | bytes 4980736 | tf_op jit(solution)/shard_map/dot_general | solution.py:23
  72.9 6.9 %all_to_all.20 = f32[2,192,1792]{2,1,0:T(8,128)} all-to-all(f32[2,192,1792]{2,1,0:T(8,128)S(1)} %bitcast.13), channel_id=1, replica_groups=mesh['groups'=2,'mp'=16,'dp'=8,'guide'=2] {'guide'}, dimensions={0} | all-to-all | bytes 5505024 | tf_op jit(solution)/shard_map/all_to_all | solution.py:8
  79.8 2.0 %reduce_sum.30 = bf16[192,1792]{1,0:T(8,128)(2,1)S(1)} reduce(f32[2,192,1792]{2,1,0:T(8,128)} %all_to_all.20, f32[]{:T(128)} %constant.4.clone.1), dimensions={0}, to_apply=%region_0.0 | reduce | flops 344064 | bytes 3440644 | tf_op jit(solution)/shard_map/reduce_sum | solution.py:9
  81.8 28.4 %all_to_all.21 = bf16[8,24,1792]{2,1,0:T(8,128)(2,1)S(1)} all-to-all(bf16[8,24,1792]{2,1,0:T(8,128)(2,1)S(1)} %bitcast.14), channel_id=1, replica_groups=mesh['groups'=2,'mp'=16,'dp'=8,'guide'=2] {'dp'}, dimensions={0} | all-to-all | bytes 1376256 | tf_op jit(solution)/shard_map/all_to_all | solution.py:8
  110.2 0.1 convert_reduce_fusion
  110.4 0.1 stack.2
  110.4 23.2 %all_to_all.22 = bf16[16,24,896]{2,1,0:T(8,128)(2,1)S(1)} all-to-all(bf16[16,24,896]{2,1,0:T(8,128)(2,1)S(1)} %stack.2), channel_id=1, replica_groups=mesh['groups'=2,'mp'=16,'dp'=8,'guide'=2] {'dp','guide'}, dimensions={0} | all-to-all | bytes 1376256 | tf_op jit(solution)/shard_map/all_to_all | solution.py:28
  133.6 0.0 copy-done
  133.6 0.6 convolution_convert_fusion
  134.2 28.9 %all_to_all.23 = bf16[16,24,512]{2,1,0:T(8,128)(2,1)S(1)} all-to-all(bf16[16,24,512]{2,1,0:T(8,128)(2,1)S(1)} %bitcast.18), channel_id=1, replica_groups=mesh['groups'=2,'mp'=16,'dp'=8,'guide'=2] {'mp'}, dimensions={0} | all-to-all | bytes 786432 | tf_op jit(solution)/shard_map/all_to_all | solution.py:8
  163.1 0.7 reduce_sum.32
  (2 shorter events, 0.1 us)
Async XLA Ops:
  0.0 133.6 %copy-start = (bf16[896,512]{1,0:T(8,128)(2,1)S(1)}, bf16[896,512]{1,0:T(8,128)(2,1)}, u32[]{:S(2)}) copy-start(bf16[896,512]{1,0:T(8,128)(2,1)} %param.7) | copy-start | bytes 2752516
